TPU v7x, 32 devices: a whole 2x2x4 slice. The times are simulated.
32 devices in a mesh: dp: 8 (over z, x), mp: 4 (over y, core).
Axes of the slice: x: 2, y: 2, z: 4, core: 2. Of those that a mesh axis runs over, the one named last changes fastest.
Arguments:
- gating_logits: bfloat16 [8, 3, 64, 7168], P('dp', None, None, 'mp'), may hold values from -6 to 6
- lifted_hidden_values: bfloat16 [8, 3, 64, 7168], P('dp', None, None, 'mp'), may hold values from -6 to 6
- loss_output_grad: bfloat16 [8, 3, 64, 2048], P('dp', None, None, 'mp'), may hold values from -160 to 160
- arrival_flags: int32 [8], P('dp'), may hold values from 0 to 1, as said below
- block_owner_map: int32 [8, 3], P('dp'), may hold values from 0 to 7, as said below
- decoder_multipliers: int32 [8, 3], P('dp'), may hold values from 1 to 4
- block_piece_number: int32 [8], replicated, may hold values from 1 to 2, as said below
Outputs:
- down_grad: float32 [2048, 7168], P('dp', 'mp')
Inputs may be any that keep to these rules, and one draw needn't show every extreme that they name: `arrival_flags`: at least one replica survives. `block_owner_map`: row i lists the partitions (i + r + k) mod 8 for k < 3, with one r for all rows. `block_piece_number`: some partition has exactly 2 live tiles.
All inputs are finite; a program needn't handle non-finite values.
Results may differ from a plain program's by a relative error of at most 0.0042.
Values may be sent and summed in bfloat16 or wider, within the bound.
A program may use at most 128 MiB of HBM per device.

v0:
```python
import jax
import jax.numpy as jnp
from jax import lax
from jax.sharding import PartitionSpec as P

TILE = 32


def slot_product(columns, hidden_k):
    return lax.dot_general(
        columns, hidden_k, (((0,), (0,)), ((), ())), preferred_element_type=jnp.float32
    )


def on_device(
    gating_logits,
    lifted_hidden_values,
    loss_output_grad,
    arrival_flags,
    block_owner_map,
    decoder_multipliers,
    block_piece_number,
):
    slot_tally = gating_logits.shape[1]
    tok_rows = gating_logits.shape[2]
    part_ids = jnp.arange(block_piece_number.shape[0], dtype=jnp.int32)
    slot_tiles = jnp.sum(
        jnp.where(block_owner_map[0][:, None] == part_ids[None, :], block_piece_number[None, :], 0),
        axis=1,
    )
    live_rows = slot_tiles * TILE
    live_mask = jnp.arange(tok_rows, dtype=jnp.int32)[None, :] < live_rows[:, None]
    hidden = (
        jax.nn.silu(gating_logits[0].astype(jnp.float32))
        * lifted_hidden_values[0].astype(jnp.float32)
        * live_mask[:, :, None].astype(jnp.float32)
    ).astype(jnp.bfloat16)
    down_kernel_array = arrival_flags[0].astype(jnp.float32) * decoder_multipliers[0].astype(
        jnp.float32
    )
    token_sum = jnp.sum(down_kernel_array * live_rows.astype(jnp.float32))
    cotangent = lax.all_gather(loss_output_grad, "mp", axis=3, tiled=True)[0]
    feature_total = cotangent.shape[2]
    block_count = 8
    block_rows = feature_total // block_count

    def project(carry, block_num):
        columns = lax.dynamic_slice_in_dim(cotangent, block_num * block_rows, block_rows, 2)
        running_total = jnp.zeros((block_rows, hidden.shape[2]), jnp.float32)
        for slot_num in range(slot_tally):
            product = slot_product(columns[slot_num], hidden[slot_num])
            running_total = running_total + down_kernel_array[slot_num] * product
        return (carry, running_total)

    _, blocks = lax.scan(
        project, jnp.zeros((), jnp.float32), jnp.arange(block_count, dtype=jnp.int32)
    )
    gradient = blocks.reshape(feature_total, hidden.shape[2])
    replicas = lax.axis_size("dp")
    stacked = gradient.reshape(replicas, feature_total // replicas, hidden.shape[2])
    received = lax.all_to_all(stacked, "dp", split_axis=0, concat_axis=0, tiled=True)
    total_tokens = lax.psum(token_sum, "dp")
    return jnp.sum(received, axis=0) / total_tokens


def solution(mesh):
    return jax.shard_map(
        on_device,
        mesh=mesh,
        in_specs=(
            P("dp", None, None, "mp"),
            P("dp", None, None, "mp"),
            P("dp", None, None, "mp"),
            P("dp"),
            P("dp", None),
            P("dp", None),
            P(),
        ),
        out_specs=P("dp", "mp"),
        check_vma=False,
    )
```

profile of v0, /device:TPU:0, one launch (start us, length us, event | category | flops | bytes accessed | tf_op | source)
XLA Modules:
  0.0 420.8 jit_solution(8810284644568872122)
XLA Ops:
  0.7 0.9 select_reduce_fusion
  1.6 10.3 %all_gather.3 = bf16[1,3,64,2048]{3,2,1,0:T(8,128)(2,1)S(1)} all-gather(bf16[1,3,64,512]{3,2,1,0:T(8,128)(2,1)} %param.11), channel_id=1, replica_groups=mesh['dp'=8,'mp'=4] {'mp'}, dimensions={3}, use_global_device_ids=true | all-gather | bytes 983040 | tf_op jit(solution)/shard_map/all_gather | solution.py:42
  11.9 1.3 multiply_reduce_fusion
  13.2 1.8 fusion.18
  15.0 73.1 %while.10 = (s32[]{:T(128)}, f32[8,256,1792]{2,1,0:T(8,128)}, f32[3]{0:T(128)S(1)}, s32[8]{0:T(128)S(1)}, bf16[3,64,2048]{2,1,0:T(8,128)(2,1)S(1)}, /*index=5*/b...) while((s32[]{:T(128)}, f32[8,256,1792]{2,1,0:T(8,128)}, ...), condition=%wide.region_2.3_spmd, body=%wide.region_1.2_spmd.sunk | while | flops 178454528 | bytes 9962747 | solution.py:55
  15.0 0.6 dynamic_slice.8
  16.3 0.7 fusion.30
  16.9 2.4 convolution_multiply_fusion.4
  19.3 2.5 fusion.31
  21.8 2.3 fusion.32
  24.2 0.6 dynamic_slice.8
  25.4 0.7 fusion.30
  26.1 2.3 convolution_multiply_fusion.4
  28.4 2.6 fusion.31
  31.0 2.3 fusion.32
  33.3 0.6 dynamic_slice.8
  34.5 0.7 fusion.30
  35.2 2.3 convolution_multiply_fusion.4
  37.5 2.5 fusion.31
  40.1 2.3 fusion.32
  42.4 0.6 dynamic_slice.8
  43.6 0.7 fusion.30
  44.3 2.3 convolution_multiply_fusion.4
  46.7 2.6 fusion.31
  49.2 2.4 fusion.32
  51.6 0.6 dynamic_slice.8
  52.8 0.7 fusion.30
  53.5 2.3 convolution_multiply_fusion.4
  55.8 2.5 fusion.31
  58.4 2.4 fusion.32
  62.0 0.7 fusion.30
  62.7 2.3 convolution_multiply_fusion.4
  65.0 2.5 fusion.31
  67.6 2.3 fusion.32
  71.1 0.7 fusion.30
  71.8 2.3 convolution_multiply_fusion.4
  74.1 2.6 fusion.31
  76.7 2.3 fusion.32
  79.0 0.6 dynamic_slice.8
  80.2 0.7 fusion.30
  80.9 2.3 convolution_multiply_fusion.4
  83.3 2.6 fusion.31
  85.8 2.3 fusion.32
  88.1 5.8 %all-to-all-start = ((f32[8,256,1792]{2,1,0:T(8,128)}), f32[8,256,1792]{2,1,0:T(8,128)}, u32[]{:S(2)}, u32[]{:S(2)}) async-start(f32[8,256,1792]{2,1,0:T(8,128)} %get-tuple-element.37), calls=%async_computation | async-start | bytes 29360128 | tf_op jit(solution)/shard_map/all_to_all | solution.py:61
  93.9 253.7 %psum.7 = f32[]{:T(128)} all-reduce(f32[]{:T(128)} %get-tuple-element.50), channel_id=1, replica_groups=mesh['dp'=8,'mp'=4] {'dp'}, use_global_device_ids=true, to_apply=%region_5.6 | all-reduce | flops 1 | bytes 8 | tf_op jit(solution)/shard_map/psum | solution.py:62
  347.6 64.9 %all-to-all-done = f32[8,256,1792]{2,1,0:T(8,128)} async-done(((f32[8,256,1792]{2,1,0:T(8,128)}), f32[8,256,1792]{2,1,0:T(8,128)}, u32[]{:S(2)}, u32[]{:S(2)}) %all-to-all-start) | async-done | bytes 14680096 | tf_op jit(solution)/shard_map/all_to_all | solution.py:61
  412.6 6.3 %reduce_sum.28 = f32[256,1792]{1,0:T(8,128)S(1)} reduce(f32[8,256,1792]{2,1,0:T(8,128)} %all-to-all-done, f32[]{:T(128)} %constant.7.clone.1), dimensions={0}, to_apply=%region_3.4 | reduce | flops 3211264 | bytes 16515076 | tf_op jit(solution)/shard_map/reduce_sum | solution.py:63
  418.8 2.0 broadcast_divide_fusion
  (6 shorter events, 1.2 us)
Async XLA Ops:
  88.1 324.4 %all-to-all-start = ((f32[8,256,1792]{2,1,0:T(8,128)}), f32[8,256,1792]{2,1,0:T(8,128)}, u32[]{:S(2)}, u32[]{:S(2)}) async-start(f32[8,256,1792]{2,1,0:T(8,128)} %get-tuple-element.37), calls=%async_computation | async-start | bytes 29360128 | tf_op jit(solution)/shard_map/all_to_all | solution.py:61
where the time goes:
time: 429 us; the launch traced here: 421 us
  blocking collectives  264 us (62%)
  waiting for transfers between devices  64.9 us (15%)
  matrix products  57.8 us (13%)
  other arithmetic  12.3 us (3%)
  local copies, waits for them, and re-layouts  10 us (2%)
  starting transfers between devices  5.79 us (1%)
  loops' own time  5.34 us (1%)
    psum x1, blocking collectives, on_device(): total_tokens = lax.psum(token_sum, 'dp')  254 us
    all_to_all x1, waiting for transfers between devices, on_device(): lax.all_to_all(stacked, 'dp', split_axis=0, concat_axis=0, tiled=True)  64.9 us
    dot_general x24, matrix products, slot_product(): lax.dot_general(columns, hidden_k, (((0,), (0,)), ((), ())), preferred_el...  57.8 us
    all_gather x1, blocking collectives, on_device(): cotangent = lax.all_gather(loss_output_grad, 'mp', axis=3, tiled=True)[0]  10.3 us
  transfers between devices with their start and end apart: 1, of which 1 were waited for; matrix products, arithmetic and copies ran while one was open for 0% of the time, Pallas kernels for 0%

commit v1 on v0

v1 whole, which is shorter than its diff:
```python
import functools

import jax
import jax.numpy as jnp
from jax import lax
from jax.experimental import pallas as pl
from jax.experimental.pallas import tpu as pltpu
from jax.sharding import PartitionSpec as P

TILE = 32
CHUNK = 256


def kernel(
    sizes,
    flags_ref,
    owner_ref,
    mult_ref,
    pieces_ref,
    gate_ref,
    lift_ref,
    cot_ref,
    out_ref,
    hid,
    cot_all,
    cot_t,
    part,
    arrived,
    tok_mine,
    tok_g,
    tok_sum,
    tok_r,
    send_c,
    recv_c,
    send_h,
    recv_h,
    send_p,
    recv_p,
    send_tg,
    recv_tg,
    send_tr,
    recv_tr,
):
    G, R, M, slots, toks, chunks, rows = sizes
    d = lax.axis_index("dp")
    m = lax.axis_index("mp")
    g = d // R
    r = d % R
    own_cot = g == m

    def dev(g_to, r_to, m_to):
        return {"dp": g_to * R + r_to, "mp": m_to}

    def remote(src, dst, s, q, where):
        return pltpu.make_async_remote_copy(
            src_ref=src,
            dst_ref=dst,
            send_sem=s,
            recv_sem=q,
            device_id=where,
            device_id_type=pl.DeviceIdType.MESH,
        )

    def cot_copy(m_to):
        return remote(cot_ref, cot_all.at[g], send_c.at[m_to], recv_c.at[g], dev(m, r, m_to))

    def cot_in(g_from):
        return remote(
            cot_ref, cot_all.at[g_from], send_c.at[0], recv_c.at[g_from], dev(g_from, r, g)
        )

    def hid_copy(c, off):
        return remote(
            hid.at[c, g],
            hid.at[c, g],
            send_h.at[c, off],
            recv_h.at[c, g],
            dev((g + off) % G, r, m),
        )

    def hid_in(c, off):
        g_from = (g + off) % G
        return remote(
            hid.at[c, g_from],
            hid.at[c, g_from],
            send_h.at[c, off],
            recv_h.at[c, g_from],
            dev(g_from, r, m),
        )

    def part_copy(c, off):
        r_to = (r + off) % R
        return remote(
            part.at[c, r_to], arrived.at[c, r], send_p.at[c, off], recv_p.at[c, r], dev(g, r_to, m)
        )

    def part_in(c, off):
        r_from = (r + off) % R
        return remote(
            part.at[c, r_from],
            arrived.at[c, r_from],
            send_p.at[c, off],
            recv_p.at[c, r_from],
            dev(g, r_from, m),
        )

    def tok_copy(off):
        return remote(
            tok_mine, tok_g.at[g], send_tg.at[off], recv_tg.at[g], dev((g + off) % G, r, m)
        )

    def tok_in(off):
        g_from = (g + off) % G
        return remote(
            tok_mine, tok_g.at[g_from], send_tg.at[off], recv_tg.at[g_from], dev(g_from, r, m)
        )

    def sum_copy(off):
        return remote(
            tok_sum, tok_r.at[r], send_tr.at[off], recv_tr.at[r], dev(g, (r + off) % R, m)
        )

    def sum_in(off):
        r_from = (r + off) % R
        return remote(
            tok_sum, tok_r.at[r_from], send_tr.at[off], recv_tr.at[r_from], dev(g, r_from, m)
        )

    def over_r(body):
        def step(off, carry):
            body(off)
            return carry

        lax.fori_loop(1, R, step, 0)

    barrier = pltpu.get_barrier_semaphore()

    def greet(where):
        pl.semaphore_signal(
            barrier, inc=1, device_id=where, device_id_type=pl.DeviceIdType.MESH
        )

    for i in range(G):

        @pl.when(jnp.logical_not(jnp.logical_and(own_cot, i == g)))
        def _():
            greet(dev(i, r, g))

    for off in range(1, G):
        greet(dev((g + off) % G, r, m))
    over_r(lambda off: greet(dev(g, (r + off) % R, m)))
    pl.semaphore_wait(barrier, M + G - 1 + R - 1 - own_cot.astype(jnp.int32))

    for i in range(M):

        @pl.when(jnp.logical_not(jnp.logical_and(own_cot, i == m)))
        def _():
            cot_copy(i).start()

    @pl.when(own_cot)
    def _():
        cot_all[g] = cot_ref[...]

    flag = flags_ref[0].astype(jnp.float32)
    scales = []
    token_sum = jnp.float32(0)
    row = lax.broadcasted_iota(jnp.int32, (toks, CHUNK), 0)
    for k in range(slots):
        live = pieces_ref[owner_ref[0, k]] * TILE
        weight = flag * mult_ref[0, k].astype(jnp.float32)
        scales.append(jnp.where(row < live, weight, 0.0))
        token_sum = token_sum + weight * live.astype(jnp.float32)

    for c in range(chunks):
        cols = pl.ds(c * CHUNK, CHUNK)
        for k in range(slots):
            rk = pl.ds(k * toks, toks)
            v = gate_ref[rk, cols].astype(jnp.float32)
            u = lift_ref[rk, cols].astype(jnp.float32)
            h = v / (1.0 + jnp.exp(-v)) * u * scales[k]
            hid[c, g, rk, :] = h.astype(jnp.bfloat16)
        if c == 0:
            tok_mine[...] = jnp.full(tok_mine.shape, token_sum, jnp.float32)
        for off in range(1, G):
            hid_copy(c, off).start()
        if c == 0:
            for off in range(1, G):
                tok_copy(off).start()

    for i in range(G):

        @pl.when(jnp.logical_not(jnp.logical_and(own_cot, i == g)))
        def _():
            cot_in(i).wait_recv()

    for i in range(G):
        n = slots * toks
        cot_t[:, pl.ds(i * n, n)] = cot_all[i].T

    for c in range(chunks):
        for off in range(1, G):
            hid_in(c, off).wait_recv()
        block = hid[c].reshape(G * slots * toks, CHUNK)
        if c == 0:
            total = tok_mine[...]
            for off in range(1, G):
                tok_in(off).wait_recv()
                total = total + tok_g[(g + off) % G]
            tok_sum[...] = total

        def other(off):
            r_to = (r + off) % R
            left = cot_t[pl.ds(pl.multiple_of(r_to * rows, rows), rows), :]
            prod = jnp.dot(left, block, preferred_element_type=jnp.float32)
            part[c, r_to] = prod.astype(jnp.bfloat16)
            part_copy(c, off).start()

        over_r(other)
        if c == 0:
            over_r(lambda off: sum_copy(off).start())
        left = cot_t[pl.ds(pl.multiple_of(r * rows, rows), rows), :]
        out_ref[:, pl.ds(c * CHUNK, CHUNK)] = jnp.dot(
            left, block, preferred_element_type=jnp.float32
        )

    def add_tokens(off, total):
        sum_in(off).wait_recv()
        return total + tok_r[(r + off) % R]

    total = lax.fori_loop(1, R, add_tokens, tok_sum[...])
    inverse = (1.0 / total)[0:1, 0:1]
    for c in range(chunks):
        cols = pl.ds(c * CHUNK, CHUNK)

        def add_part(off):
            part_in(c, off).wait_recv()
            out_ref[:, cols] = out_ref[:, cols] + arrived[c, (r + off) % R].astype(jnp.float32)

        over_r(add_part)
        out_ref[:, cols] = out_ref[:, cols] * inverse

    for i in range(M):

        @pl.when(jnp.logical_not(jnp.logical_and(own_cot, i == m)))
        def _():
            cot_copy(i).wait_send()

    for off in range(1, G):
        tok_copy(off).wait_send()
        for c in range(chunks):
            hid_copy(c, off).wait_send()

    def drain(off):
        sum_copy(off).wait_send()
        for c in range(chunks):
            part_copy(c, off).wait_send()

    over_r(drain)


def on_device(
    mesh_shape,
    gating_logits,
    lifted_hidden_values,
    loss_output_grad,
    arrival_flags,
    block_owner_map,
    decoder_multipliers,
    block_piece_number,
):
    dp, M = mesh_shape
    G = M
    R = dp // G
    _, slots, toks, width = gating_logits.shape
    feats = loss_output_grad.shape[3]
    rows = feats * M // dp
    chunks = width // CHUNK
    n = slots * toks
    sizes = (G, R, M, slots, toks, chunks, rows)
    smem = pl.BlockSpec(memory_space=pltpu.SMEM)
    vmem = pl.BlockSpec(memory_space=pltpu.VMEM)
    dma = pltpu.SemaphoreType.DMA
    bf, f32 = jnp.bfloat16, jnp.float32
    return pl.pallas_call(
        functools.partial(kernel, sizes),
        out_shape=jax.ShapeDtypeStruct((rows, width), f32),
        in_specs=[smem] * 4 + [vmem] * 3,
        out_specs=vmem,
        scratch_shapes=[
            pltpu.VMEM((chunks, G, n, CHUNK), bf),
            pltpu.VMEM((G, n, feats), bf),
            pltpu.VMEM((feats, G * n), bf),
            pltpu.VMEM((chunks, R, rows, CHUNK), bf),
            pltpu.VMEM((chunks, R, rows, CHUNK), bf),
            pltpu.VMEM((8, 128), f32),
            pltpu.VMEM((G, 8, 128), f32),
            pltpu.VMEM((8, 128), f32),
            pltpu.VMEM((R, 8, 128), f32),
            dma((M,)),
            dma((G,)),
            dma((chunks, G)),
            dma((chunks, G)),
            dma((chunks, R)),
            dma((chunks, R)),
            dma((G,)),
            dma((G,)),
            dma((R,)),
            dma((R,)),
        ],
        compiler_params=pltpu.CompilerParams(
            collective_id=0, has_side_effects=True, vmem_limit_bytes=48 * 1024 * 1024
        ),
    )(
        arrival_flags,
        block_owner_map,
        decoder_multipliers,
        block_piece_number,
        gating_logits.reshape(n, width),
        lifted_hidden_values.reshape(n, width),
        loss_output_grad.reshape(n, feats),
    )


def solution(mesh):
    shape = (mesh.shape["dp"], mesh.shape["mp"])
    return jax.shard_map(
        functools.partial(on_device, shape),
        mesh=mesh,
        in_specs=(
            P("dp", None, None, "mp"),
            P("dp", None, None, "mp"),
            P("dp", None, None, "mp"),
            P("dp"),
            P("dp", None),
            P("dp", None),
            P(),
        ),
        out_specs=P("dp", "mp"),
        check_vma=False,
    )
```

time: 429 us -> 112 us (0.26); the launches traced: 421 us -> 112 us
  blocking collectives: 264 us -> 0 us
  Pallas kernels: 0 us -> 105 us
  waiting for transfers between devices: 64.9 us -> 0 us
  matrix products: 57.8 us -> 0 us
  other arithmetic: 12.3 us -> 0 us
  starting transfers between devices: 5.79 us -> 0 us
  loops' own time: 5.34 us -> 0 us
    psum x1 -> x0, blocking collectives: 254 us -> none  [on_device(): total_tokens = lax.psum(token_sum, 'dp')]
    pallas_call x0 -> x1, Pallas kernels: none -> 105 us  [on_device(): pl.pallas_call(functools.partial(kernel, sizes), out_shape=jax.ShapeDtype...]
    all_to_all x1 -> x0, waiting for transfers between devices: 64.9 us -> none  [on_device(): lax.all_to_all(stacked, 'dp', split_axis=0, concat_axis=0, tiled=True)]
    dot_general x24 -> x0, matrix products: 57.8 us -> none  [slot_product(): lax.dot_general(columns, hidden_k, (((0,), (0,)), ((), ())), preferred_el...]
    all_gather x1 -> x0, blocking collectives: 10.3 us -> none  [on_device(): cotangent = lax.all_gather(loss_output_grad, 'mp', axis=3, tiled=True)[0]]
    reduce_sum x3 -> x0, other arithmetic: 8.45 us -> none  [the longest x1 6.27 us: on_device(): return jnp.sum(received, axis=0) / total_tokens]
    unnamed x0 -> x13, local copies, waits for them, and re-layouts: none -> 6.31 us
    all_to_all x1 -> x0, starting transfers between devices: 5.79 us -> none  [on_device(): lax.all_to_all(stacked, 'dp', split_axis=0, concat_axis=0, tiled=True)]
  transfers between devices with their start and end apart: 1 -> 0, of which waited for: 1 -> 0; matrix products, arithmetic and copies ran while one was open for 0% -> 0% of each run, Pallas kernels for 0% -> 0%
where the time goes in v1:
time: 112 us
  Pallas kernels  105 us (94%)
  local copies, waits for them, and re-layouts  6.31 us (6%)
    pallas_call x1, Pallas kernels, on_device(): pl.pallas_call(functools.partial(kernel, sizes), out_shape=jax.ShapeDtype...  105 us
    unnamed x13, local copies, waits for them, and re-layouts  6.31 us

profile of v1, /device:TPU:0, one launch (start us, length us, event | category | flops | bytes accessed | tf_op | source)
XLA Modules:
  0.0 111.6 jit_solution(15649015681106753097)
XLA Ops:
  0.7 0.0 copy-start
  0.7 1.1 copy-done
  1.8 0.0 copy-start.1
  1.8 1.1 copy-done.1
  2.9 0.0 copy-start.2
  2.9 0.9 copy-done.2
  3.8 0.0 copy-start.3
  3.8 0.7 copy-done.3
  4.4 0.0 copy-start.4
  4.4 0.7 copy-done.4
  5.1 0.0 copy-start.5
  5.1 0.7 copy-done.5
  5.7 104.6 %shard_map.73 = f32[256,1792]{1,0:T(8,128)S(1)} custom-call(s32[1]{0:T(128)S(6)} %copy.9.flags_ref, s32[1,3]{1,0:T(1,128)S(1)} %copy-done.3, s32[1,3]{1,0:T(1,128)S(1)} %copy-done.4, s32[8]{0:T(128)S(1)} %copy-done.5, bf16[192,1792]{1,0:T(8,128)(2,1)S(1)} %bitcast.3, bf16[192,1792]{1,0:T(8,128)(2,1)S(1)} %bitcast.4, bf16[192,512]{1,0:T(8,128)(2,1)S(1)} %bitcast.5), custom_call_target="tpu_custom_call" | custom-call | tf_op jit(solution)/shard_map/pallas_call | solution.py:284
  110.4 1.2 %copy.10 = f32[256,1792]{1,0:T(8,128)} copy(f32[256,1792]{1,0:T(8,128)S(1)} %shard_map.73) | data formatting | bytes 3670016
Async XLA Ops:
  0.7 1.1 copy-start
  1.8 1.1 copy-start.1
  2.9 0.9 copy-start.2
  3.8 0.7 copy-start.3
  4.4 0.7 copy-start.4
  5.1 0.7 copy-start.5

commit v2 on v1

--- a/solution.py
+++ b/solution.py
@@ -17,10 +17,14 @@
     owner_ref,
     mult_ref,
     pieces_ref,
-    gate_ref,
-    lift_ref,
+    gate_hbm,
+    lift_hbm,
+    cot_hbm,
+    out_ref,
+    gate_in,
+    lift_in,
     cot_ref,
-    out_ref,
+    quarters,
     hid,
     cot_all,
     cot_t,
@@ -30,8 +34,15 @@
     tok_g,
     tok_sum,
     tok_r,
-    send_c,
-    recv_c,
+    load_c,
+    load_g,
+    load_l,
+    send_1,
+    recv_1,
+    send_2,
+    recv_2,
+    send_3,
+    recv_3,
     send_h,
     recv_h,
     send_p,
@@ -46,7 +57,7 @@
     m = lax.axis_index("mp")
     g = d // R
     r = d % R
-    own_cot = g == m
+    quarter = slots * toks // M
 
     def dev(g_to, r_to, m_to):
         return {"dp": g_to * R + r_to, "mp": m_to}
@@ -61,12 +72,60 @@
             device_id_type=pl.DeviceIdType.MESH,
         )
 
-    def cot_copy(m_to):
-        return remote(cot_ref, cot_all.at[g], send_c.at[m_to], recv_c.at[g], dev(m, r, m_to))
-
-    def cot_in(g_from):
-        return remote(
-            cot_ref, cot_all.at[g_from], send_c.at[0], recv_c.at[g_from], dev(g_from, r, g)
+    def spread_copy(off):
+        m_to = (m + off) % M
+        return remote(
+            cot_ref.at[pl.ds(pl.multiple_of(m_to * quarter, quarter), quarter)],
+            quarters.at[m],
+            send_1.at[off],
+            recv_1.at[m],
+            dev(g, r, m_to),
+        )
+
+    def spread_in(off):
+        m_from = (m + off) % M
+        return remote(
+            quarters.at[m_from],
+            quarters.at[m_from],
+            send_1.at[off],
+            recv_1.at[m_from],
+            dev(g, r, m_from),
+        )
+
+    def cross_copy(off):
+        g_to = (g + off) % G
+        return remote(
+            quarters.at[g_to], cot_all.at[m, g], send_2.at[off], recv_2.at[g], dev(g_to, r, m)
+        )
+
+    def cross_in(off):
+        g_from = (g + off) % G
+        return remote(
+            quarters.at[g],
+            cot_all.at[m, g_from],
+            send_2.at[off],
+            recv_2.at[g_from],
+            dev(g_from, r, m),
+        )
+
+    def share_copy(off):
+        return remote(
+            cot_all.at[m], cot_all.at[m], send_3.at[off], recv_3.at[m], dev(g, r, (m + off) % M)
+        )
+
+    def share_in(off):
+        m_from = (m + off) % M
+        return remote(
+            cot_all.at[m_from],
+            cot_all.at[m_from],
+            send_3.at[off],
+            recv_3.at[m_from],
+            dev(g, r, m_from),
+        )
+
+    def load(src, dst, c, sem):
+        return pltpu.make_async_copy(
+            src.at[:, pl.ds(c * CHUNK, CHUNK)], dst.at[c], sem.at[c]
         )
 
     def hid_copy(c, off):
@@ -133,6 +192,12 @@
 
         lax.fori_loop(1, R, step, 0)
 
+    load_cot = pltpu.make_async_copy(cot_hbm, cot_ref, load_c)
+    load_cot.start()
+    for c in range(chunks):
+        load(gate_hbm, gate_in, c, load_g).start()
+        load(lift_hbm, lift_in, c, load_l).start()
+
     barrier = pltpu.get_barrier_semaphore()
 
     def greet(where):
@@ -140,26 +205,17 @@
             barrier, inc=1, device_id=where, device_id_type=pl.DeviceIdType.MESH
         )
 
-    for i in range(G):
-
-        @pl.when(jnp.logical_not(jnp.logical_and(own_cot, i == g)))
-        def _():
-            greet(dev(i, r, g))
-
+    for off in range(1, M):
+        greet(dev(g, r, (m + off) % M))
     for off in range(1, G):
         greet(dev((g + off) % G, r, m))
     over_r(lambda off: greet(dev(g, (r + off) % R, m)))
-    pl.semaphore_wait(barrier, M + G - 1 + R - 1 - own_cot.astype(jnp.int32))
-
-    for i in range(M):
-
-        @pl.when(jnp.logical_not(jnp.logical_and(own_cot, i == m)))
-        def _():
-            cot_copy(i).start()
-
-    @pl.when(own_cot)
-    def _():
-        cot_all[g] = cot_ref[...]
+    load_cot.wait()
+    quarters[m] = cot_ref[pl.ds(pl.multiple_of(m * quarter, quarter), quarter), :]
+    pl.semaphore_wait(barrier, M - 1 + G - 1 + R - 1)
+
+    for off in range(1, M):
+        spread_copy(off).start()
 
     flag = flags_ref[0].astype(jnp.float32)
     scales = []
@@ -172,11 +228,12 @@
         token_sum = token_sum + weight * live.astype(jnp.float32)
 
     for c in range(chunks):
-        cols = pl.ds(c * CHUNK, CHUNK)
+        load(gate_hbm, gate_in, c, load_g).wait()
+        load(lift_hbm, lift_in, c, load_l).wait()
         for k in range(slots):
             rk = pl.ds(k * toks, toks)
-            v = gate_ref[rk, cols].astype(jnp.float32)
-            u = lift_ref[rk, cols].astype(jnp.float32)
+            v = gate_in[c, rk, :].astype(jnp.float32)
+            u = lift_in[c, rk, :].astype(jnp.float32)
             h = v / (1.0 + jnp.exp(-v)) * u * scales[k]
             hid[c, g, rk, :] = h.astype(jnp.bfloat16)
         if c == 0:
@@ -186,16 +243,23 @@
         if c == 0:
             for off in range(1, G):
                 tok_copy(off).start()
-
-    for i in range(G):
-
-        @pl.when(jnp.logical_not(jnp.logical_and(own_cot, i == g)))
-        def _():
-            cot_in(i).wait_recv()
+            for off in range(1, M):
+                spread_in(off).wait_recv()
+            cot_all[m, g] = quarters[g]
+            for off in range(1, G):
+                cross_copy(off).start()
+
+    for off in range(1, G):
+        cross_in(off).wait_recv()
+    for off in range(1, M):
+        share_copy(off).start()
+    for off in range(1, M):
+        share_in(off).wait_recv()
 
     for i in range(G):
         n = slots * toks
-        cot_t[:, pl.ds(i * n, n)] = cot_all[i].T
+        block = jnp.concatenate([cot_all[j, i] for j in range(M)], axis=0)
+        cot_t[:, pl.ds(i * n, n)] = block.T
 
     for c in range(chunks):
         for off in range(1, G):
@@ -239,14 +303,13 @@
         over_r(add_part)
         out_ref[:, cols] = out_ref[:, cols] * inverse
 
-    for i in range(M):
-
-        @pl.when(jnp.logical_not(jnp.logical_and(own_cot, i == m)))
-        def _():
-            cot_copy(i).wait_send()
+    for off in range(1, M):
+        spread_copy(off).wait_send()
+        share_copy(off).wait_send()
 
     for off in range(1, G):
         tok_copy(off).wait_send()
+        cross_copy(off).wait_send()
         for c in range(chunks):
             hid_copy(c, off).wait_send()
 
@@ -284,11 +347,15 @@
     return pl.pallas_call(
         functools.partial(kernel, sizes),
         out_shape=jax.ShapeDtypeStruct((rows, width), f32),
-        in_specs=[smem] * 4 + [vmem] * 3,
+        in_specs=[smem] * 4 + [pl.BlockSpec(memory_space=pl.ANY)] * 3,
         out_specs=vmem,
         scratch_shapes=[
+            pltpu.VMEM((chunks, n, CHUNK), bf),
+            pltpu.VMEM((chunks, n, CHUNK), bf),
+            pltpu.VMEM((n, feats), bf),
+            pltpu.VMEM((M, n // M, feats), bf),
             pltpu.VMEM((chunks, G, n, CHUNK), bf),
-            pltpu.VMEM((G, n, feats), bf),
+            pltpu.VMEM((M, G, n // M, feats), bf),
             pltpu.VMEM((feats, G * n), bf),
             pltpu.VMEM((chunks, R, rows, CHUNK), bf),
             pltpu.VMEM((chunks, R, rows, CHUNK), bf),
@@ -296,8 +363,15 @@
             pltpu.VMEM((G, 8, 128), f32),
             pltpu.VMEM((8, 128), f32),
             pltpu.VMEM((R, 8, 128), f32),
+            dma,
+            dma((chunks,)),
+            dma((chunks,)),
+            dma((M,)),
             dma((M,)),
             dma((G,)),
+            dma((G,)),
+            dma((M,)),
+            dma((M,)),
             dma((chunks, G)),
             dma((chunks, G)),
             dma((chunks, R)),
@@ -308,7 +382,7 @@
             dma((R,)),
         ],
         compiler_params=pltpu.CompilerParams(
-            collective_id=0, has_side_effects=True, vmem_limit_bytes=48 * 1024 * 1024
+            collective_id=0, has_side_effects=True
         ),
     )(
         arrival_flags,

time: 112 us -> 80.6 us (0.72)
  Pallas kernels: 105 us -> 76.9 us
  local copies, waits for them, and re-layouts: 6.31 us -> 2.85 us
    pallas_call x1, Pallas kernels: 105 us -> 76.9 us  [on_device(): pl.pallas_call(functools.partial(kernel, sizes), out_shape=jax.ShapeDtype...]
    unnamed x13 -> x1, local copies, waits for them, and re-layouts: 6.31 us -> 2.85 us
where the time goes in v2:
time: 80.6 us; the launch traced here: 80.4 us
  Pallas kernels  76.9 us (95%)
  local copies, waits for them, and re-layouts  2.85 us (4%)
    pallas_call x1, Pallas kernels, on_device(): pl.pallas_call(functools.partial(kernel, sizes), out_shape=jax.ShapeDtype...  76.9 us
    unnamed x1, local copies, waits for them, and re-layouts  2.85 us

profile of v2, /device:TPU:0, one launch (start us, length us, event | category | flops | bytes accessed | tf_op | source)
XLA Modules:
  0.0 80.4 jit_solution(16123181052973617030)
XLA Ops:
  0.7 76.9 %shard_map.73 = f32[256,1792]{1,0:T(8,128)} custom-call(s32[1]{0:T(128)S(6)} %copy.9.flags_ref, s32[1,3]{1,0:T(1,128)} %owner_ref.1, s32[1,3]{1,0:T(1,128)} %mult_ref.1, s32[8]{0:T(128)} %pieces_ref.1, bf16[192,1792]{1,0:T(8,128)(2,1)} %bitcast.3, bf16[192,1792]{1,0:T(8,128)(2,1)} %bitcast.4, bf16[192,512]{1,0:T(8,128)(2,1)} %bitcast.5), custom_call_target="tpu_custom_call" | custom-call | tf_op jit(solution)/shard_map/pallas_call | solution.py:347
  77.6 2.8 %copy.10 = f32[256,1792]{1,0:T(8,128)} copy(f32[256,1792]{1,0:T(8,128)} %shard_map.73) | data formatting | bytes 3670016

commit v3 on v2

--- a/solution.py
+++ b/solution.py
@@ -43,7 +43,8 @@
     recv_2,
     send_3,
     recv_3,
-    send_h,
+    send_up,
+    send_dn,
     recv_h,
     send_p,
     recv_p,
@@ -128,24 +129,23 @@
             src.at[:, pl.ds(c * CHUNK, CHUNK)], dst.at[c], sem.at[c]
         )
 
-    def hid_copy(c, off):
-        return remote(
-            hid.at[c, g],
-            hid.at[c, g],
-            send_h.at[c, off],
-            recv_h.at[c, g],
-            dev((g + off) % G, r, m),
-        )
-
-    def hid_in(c, off):
-        g_from = (g + off) % G
-        return remote(
-            hid.at[c, g_from],
-            hid.at[c, g_from],
-            send_h.at[c, off],
-            recv_h.at[c, g_from],
-            dev(g_from, r, m),
-        )
+    def hop(c, origin, to, sems):
+        return remote(
+            hid.at[c, origin],
+            hid.at[c, origin],
+            sems.at[c, origin],
+            recv_h.at[c, origin],
+            dev(to, r, m),
+        )
+
+    up, down = (g + 1) % G, (g + G - 1) % G
+
+    def pass_on(c, origin, has_next, to, sems):
+        hop(c, origin, to, sems).wait_recv()
+
+        @pl.when(has_next)
+        def _():
+            hop(c, origin, to, sems).start()
 
     def part_copy(c, off):
         r_to = (r + off) % R
@@ -238,8 +238,15 @@
             hid[c, g, rk, :] = h.astype(jnp.bfloat16)
         if c == 0:
             tok_mine[...] = jnp.full(tok_mine.shape, token_sum, jnp.float32)
-        for off in range(1, G):
-            hid_copy(c, off).start()
+
+        @pl.when(g < G - 1)
+        def _():
+            hop(c, g, up, send_up).start()
+
+        @pl.when(g > 0)
+        def _():
+            hop(c, g, down, send_dn).start()
+
         if c == 0:
             for off in range(1, G):
                 tok_copy(off).start()
@@ -262,8 +269,16 @@
         cot_t[:, pl.ds(i * n, n)] = block.T
 
     for c in range(chunks):
-        for off in range(1, G):
-            hid_in(c, off).wait_recv()
+        for k in range(1, G):
+
+            @pl.when(g >= k)
+            def _():
+                pass_on(c, (g + G - k) % G, g < G - 1, up, send_up)
+
+            @pl.when(g + k < G)
+            def _():
+                pass_on(c, (g + k) % G, g > 0, down, send_dn)
+
         block = hid[c].reshape(G * slots * toks, CHUNK)
         if c == 0:
             total = tok_mine[...]
@@ -310,8 +325,17 @@
     for off in range(1, G):
         tok_copy(off).wait_send()
         cross_copy(off).wait_send()
-        for c in range(chunks):
-            hid_copy(c, off).wait_send()
+
+    for c in range(chunks):
+        for i in range(G):
+
+            @pl.when(jnp.logical_and(i <= g, g < G - 1))
+            def _():
+                hop(c, i, up, send_up).wait_send()
+
+            @pl.when(jnp.logical_and(i >= g, g > 0))
+            def _():
+                hop(c, i, down, send_dn).wait_send()
 
     def drain(off):
         sum_copy(off).wait_send()
@@ -374,6 +398,7 @@
             dma((M,)),
             dma((chunks, G)),
             dma((chunks, G)),
+            dma((chunks, G)),
             dma((chunks, R)),
             dma((chunks, R)),
             dma((G,)),

time: 80.6 us -> 71.2 us (0.88)
  Pallas kernels: 76.9 us -> 67.6 us
    pallas_call x1, Pallas kernels: 76.9 us -> 67.6 us  [on_device(): pl.pallas_call(functools.partial(kernel, sizes), out_shape=jax.ShapeDtype...]
where the time goes in v3:
time: 71.2 us; the launch traced here: 71.1 us
  Pallas kernels  67.6 us (95%)
  local copies, waits for them, and re-layouts  2.85 us (4%)
    pallas_call x1, Pallas kernels, on_device(): pl.pallas_call(functools.partial(kernel, sizes), out_shape=jax.ShapeDtype...  67.6 us
    unnamed x1, local copies, waits for them, and re-layouts  2.85 us

profile of v3, /device:TPU:0, one launch (start us, length us, event | category | flops | bytes accessed | tf_op | source)
XLA Modules:
  0.0 71.1 jit_solution(9299322002407830843)
XLA Ops:
  0.7 67.6 %shard_map.73 = f32[256,1792]{1,0:T(8,128)} custom-call(s32[1]{0:T(128)S(6)} %copy.9.flags_ref, s32[1,3]{1,0:T(1,128)} %owner_ref.1, s32[1,3]{1,0:T(1,128)} %mult_ref.1, s32[8]{0:T(128)} %pieces_ref.1, bf16[192,1792]{1,0:T(8,128)(2,1)} %bitcast.3, bf16[192,1792]{1,0:T(8,128)(2,1)} %bitcast.4, bf16[192,512]{1,0:T(8,128)(2,1)} %bitcast.5), custom_call_target="tpu_custom_call" | custom-call | tf_op jit(solution)/shard_map/pallas_call | solution.py:371
  68.2 2.8 %copy.10 = f32[256,1792]{1,0:T(8,128)} copy(f32[256,1792]{1,0:T(8,128)} %shard_map.73) | data formatting | bytes 3670016

commit v4 on v3

--- a/solution.py
+++ b/solution.py
@@ -147,6 +147,15 @@
         def _():
             hop(c, origin, to, sems).start()
 
+    def relay(c, k):
+        @pl.when(g >= k)
+        def _():
+            pass_on(c, (g + G - k) % G, g < G - 1, up, send_up)
+
+        @pl.when(g + k < G)
+        def _():
+            pass_on(c, (g + k) % G, g > 0, down, send_dn)
+
     def part_copy(c, off):
         r_to = (r + off) % R
         return remote(
@@ -212,11 +221,6 @@
     over_r(lambda off: greet(dev(g, (r + off) % R, m)))
     load_cot.wait()
     quarters[m] = cot_ref[pl.ds(pl.multiple_of(m * quarter, quarter), quarter), :]
-    pl.semaphore_wait(barrier, M - 1 + G - 1 + R - 1)
-
-    for off in range(1, M):
-        spread_copy(off).start()
-
     flag = flags_ref[0].astype(jnp.float32)
     scales = []
     token_sum = jnp.float32(0)
@@ -227,7 +231,9 @@
         scales.append(jnp.where(row < live, weight, 0.0))
         token_sum = token_sum + weight * live.astype(jnp.float32)
 
-    for c in range(chunks):
+    tok_mine[...] = jnp.full(tok_mine.shape, token_sum, jnp.float32)
+
+    def activate(c):
         load(gate_hbm, gate_in, c, load_g).wait()
         load(lift_hbm, lift_in, c, load_l).wait()
         for k in range(slots):
@@ -236,8 +242,18 @@
             u = lift_in[c, rk, :].astype(jnp.float32)
             h = v / (1.0 + jnp.exp(-v)) * u * scales[k]
             hid[c, g, rk, :] = h.astype(jnp.bfloat16)
-        if c == 0:
-            tok_mine[...] = jnp.full(tok_mine.shape, token_sum, jnp.float32)
+
+    early = min(2, chunks)
+    for c in range(early):
+        activate(c)
+
+    pl.semaphore_wait(barrier, M - 1 + G - 1 + R - 1)
+    for off in range(1, M):
+        spread_copy(off).start()
+
+    for c in range(chunks):
+        if c >= early:
+            activate(c)
 
         @pl.when(g < G - 1)
         def _():
@@ -260,6 +276,8 @@
         cross_in(off).wait_recv()
     for off in range(1, M):
         share_copy(off).start()
+    for c in range(chunks):
+        relay(c, 1)
     for off in range(1, M):
         share_in(off).wait_recv()
 
@@ -269,16 +287,8 @@
         cot_t[:, pl.ds(i * n, n)] = block.T
 
     for c in range(chunks):
-        for k in range(1, G):
-
-            @pl.when(g >= k)
-            def _():
-                pass_on(c, (g + G - k) % G, g < G - 1, up, send_up)
-
-            @pl.when(g + k < G)
-            def _():
-                pass_on(c, (g + k) % G, g > 0, down, send_dn)
-
+        for k in range(2, G):
+            relay(c, k)
         block = hid[c].reshape(G * slots * toks, CHUNK)
         if c == 0:
             total = tok_mine[...]

time: 71.2 us -> 73.2 us (1.028)
  Pallas kernels: 67.6 us -> 69.5 us
    pallas_call x1, Pallas kernels: 67.6 us -> 69.5 us  [on_device(): pl.pallas_call(functools.partial(kernel, sizes), out_shape=jax.ShapeDtype...]
where the time goes in v4:
time: 73.2 us; the launch traced here: 73 us
  Pallas kernels  69.5 us (95%)
  local copies, waits for them, and re-layouts  2.85 us (4%)
    pallas_call x1, Pallas kernels, on_device(): pl.pallas_call(functools.partial(kernel, sizes), out_shape=jax.ShapeDtype...  69.5 us
    unnamed x1, local copies, waits for them, and re-layouts  2.85 us

profile of v4, /device:TPU:0, one launch (start us, length us, event | category | flops | bytes accessed | tf_op | source)
XLA Modules:
  0.0 73.0 jit_solution(2014149267911810653)
XLA Ops:
  0.7 69.5 %shard_map.73 = f32[256,1792]{1,0:T(8,128)} custom-call(s32[1]{0:T(128)S(6)} %copy.9.flags_ref, s32[1,3]{1,0:T(1,128)} %owner_ref.1, s32[1,3]{1,0:T(1,128)} %mult_ref.1, s32[8]{0:T(128)} %pieces_ref.1, bf16[192,1792]{1,0:T(8,128)(2,1)} %bitcast.3, bf16[192,1792]{1,0:T(8,128)(2,1)} %bitcast.4, bf16[192,512]{1,0:T(8,128)(2,1)} %bitcast.5), custom_call_target="tpu_custom_call" | custom-call | tf_op jit(solution)/shard_map/pallas_call | solution.py:381
  70.2 2.8 %copy.10 = f32[256,1792]{1,0:T(8,128)} copy(f32[256,1792]{1,0:T(8,128)} %shard_map.73) | data formatting | bytes 3670016

commit v5 on v3

--- a/solution.py
+++ b/solution.py
@@ -33,6 +33,7 @@
     tok_mine,
     tok_g,
     tok_sum,
+    tok_all,
     tok_r,
     load_c,
     load_g,
@@ -268,6 +269,23 @@
         block = jnp.concatenate([cot_all[j, i] for j in range(M)], axis=0)
         cot_t[:, pl.ds(i * n, n)] = block.T
 
+    def add_tokens(off, total):
+        sum_in(off).wait_recv()
+        return total + tok_r[(r + off) % R]
+
+    def finish(c):
+        if c == 0:
+            tok_all[...] = lax.fori_loop(1, R, add_tokens, tok_sum[...])
+        inverse = 1.0 / tok_all[0:1, 0:1]
+        cols = pl.ds(c * CHUNK, CHUNK)
+
+        def add_part(off):
+            part_in(c, off).wait_recv()
+            out_ref[:, cols] = out_ref[:, cols] + arrived[c, (r + off) % R].astype(jnp.float32)
+
+        over_r(add_part)
+        out_ref[:, cols] = out_ref[:, cols] * inverse
+
     for c in range(chunks):
         for k in range(1, G):
 
@@ -301,22 +319,11 @@
         out_ref[:, pl.ds(c * CHUNK, CHUNK)] = jnp.dot(
             left, block, preferred_element_type=jnp.float32
         )
-
-    def add_tokens(off, total):
-        sum_in(off).wait_recv()
-        return total + tok_r[(r + off) % R]
-
-    total = lax.fori_loop(1, R, add_tokens, tok_sum[...])
-    inverse = (1.0 / total)[0:1, 0:1]
-    for c in range(chunks):
-        cols = pl.ds(c * CHUNK, CHUNK)
-
-        def add_part(off):
-            part_in(c, off).wait_recv()
-            out_ref[:, cols] = out_ref[:, cols] + arrived[c, (r + off) % R].astype(jnp.float32)
-
-        over_r(add_part)
-        out_ref[:, cols] = out_ref[:, cols] * inverse
+        if c >= 2:
+            finish(c - 2)
+
+    for c in range(max(chunks - 2, 0), chunks):
+        finish(c)
 
     for off in range(1, M):
         spread_copy(off).wait_send()
@@ -386,6 +393,7 @@
             pltpu.VMEM((8, 128), f32),
             pltpu.VMEM((G, 8, 128), f32),
             pltpu.VMEM((8, 128), f32),
+            pltpu.VMEM((8, 128), f32),
             pltpu.VMEM((R, 8, 128), f32),
             dma,
             dma((chunks,)),

time: 71.2 us -> 71.4 us (level)
  no operation moved by 1% of the time
where the time goes in v5:
time: 71.4 us; the launch traced here: 71.2 us
  Pallas kernels  67.7 us (95%)
  local copies, waits for them, and re-layouts  2.85 us (4%)
    pallas_call x1, Pallas kernels, on_device(): pl.pallas_call(functools.partial(kernel, sizes), out_shape=jax.ShapeDtype...  67.7 us
    unnamed x1, local copies, waits for them, and re-layouts  2.85 us

profile of v5, /device:TPU:0, one launch (start us, length us, event | category | flops | bytes accessed | tf_op | source)
XLA Modules:
  0.0 71.2 jit_solution(14128353981982627572)
XLA Ops:
  0.7 67.7 %shard_map.73 = f32[256,1792]{1,0:T(8,128)} custom-call(s32[1]{0:T(128)S(6)} %copy.9.flags_ref, s32[1,3]{1,0:T(1,128)} %owner_ref.1, s32[1,3]{1,0:T(1,128)} %mult_ref.1, s32[8]{0:T(128)} %pieces_ref.1, bf16[192,1792]{1,0:T(8,128)(2,1)} %bitcast.3, bf16[192,1792]{1,0:T(8,128)(2,1)} %bitcast.4, bf16[192,512]{1,0:T(8,128)(2,1)} %bitcast.5), custom_call_target="tpu_custom_call" | custom-call | tf_op jit(solution)/shard_map/pallas_call | solution.py:378
  68.4 2.8 %copy.10 = f32[256,1792]{1,0:T(8,128)} copy(f32[256,1792]{1,0:T(8,128)} %shard_map.73) | data formatting | bytes 3670016
